TPU v7x, 32 devices: a whole 2x2x4 slice. The times are simulated.
32 devices in a mesh: user: 8 (over z, x), pos: 4 (over y, core).
Axes of the slice: x: 2, y: 2, z: 4, core: 2. Of those that a mesh axis runs over, the one named last changes fastest.
Arguments:
- events: bfloat16 [8192, 256], P('user'), may hold values from -6 to 6
- owners: int32 [8192], P('user'), may hold values from 0 to 15, as said below
- offsets: int32 [8192], P('user'), may hold values from 0 to 2047, as said below
- w_key: bfloat16 [256, 256], replicated, may hold values from -0.375 to 0.375
- w_value: bfloat16 [256, 256], replicated, may hold values from -0.375 to 0.375
- cache_keys: bfloat16 [16, 6144, 256], P('user', 'pos'), may hold values from -7 to 7
- cache_values: bfloat16 [16, 6144, 256], P('user', 'pos'), may hold values from -6 to 6
- hist_len: int32 [16], P('user'), may hold values from 8 to 4096
- active: int32 [16], P('user'), may hold values 0 or 1
- candidates: bfloat16 [16, 1024, 256], P('user', 'pos'), may hold values from -100 to 100
Outputs:
- new_keys: bfloat16 [16, 6144, 256], P('user', 'pos')
- new_values: bfloat16 [16, 6144, 256], P('user', 'pos')
- attended: bfloat16 [16, 1024, 256], P('user', 'pos')
Inputs may be any that keep to these rules, and one draw needn't show every extreme that they name: Among the events of one aligned block of 1024 (one index of user), at most 256 have owners among the users t * 2 to t * 2 + 1, for every t; in every draw some t receives exactly 256 from every block, and all those events belong to one user of that t. offsets[e] is the number of events before e, in the order of the array, that have the same owner as e.
All inputs are finite; a program needn't handle non-finite values. No bound on the sum of `active` on one device may be relied on, other than what follows from the above.
Results may differ from a plain program's by a relative error of at most 0.0067.
Values may be sent and summed in bfloat16 or wider, within the bound.
A program may use at most 128 MiB of HBM per device.

v0:
```python
import jax
import jax.numpy as jnp
from jax import lax
from jax.sharding import PartitionSpec as P


def joined(part, axis, combine):
    gathered = jax.tree.map(lambda a: lax.all_gather(a, axis), part)

    def take(source):
        return jax.tree.map(lambda a: lax.dynamic_index_in_dim(a, source, 0, False), gathered)

    return lax.fori_loop(
        1, lax.axis_size(axis), lambda source, state: combine(state, take(source)), take(0)
    )


def join_partials(left, right):
    top = jnp.maximum(left[0], right[0])
    left_factor = jnp.exp(left[0] - top)
    right_factor = jnp.exp(right[0] - top)
    total = left[1] * left_factor + right[1] * right_factor
    acc = left[2] * left_factor[..., None] + right[2] * right_factor[..., None]
    return (top, total, acc)


def on_device(
    events, owners, offsets, w_key, w_value, cache_keys, cache_values, hist_len, active, candidates
):
    groups = lax.axis_size("user")
    blocks = lax.axis_size("pos")
    users_here = cache_keys.shape[0]
    block_rows = cache_keys.shape[1]
    width = cache_keys.shape[2]
    span = block_rows * blocks
    per_event = events.shape[0]
    capacity = 2 * per_event // groups
    slots = groups * capacity
    dest = owners // users_here
    local_user = owners - dest * users_here
    onehot = (dest[:, None] == jnp.arange(groups, dtype=jnp.int32)[None, :]).astype(jnp.int32)
    rank = jnp.sum(jnp.cumsum(onehot, axis=0) * onehot, axis=1) - 1
    slot = dest * capacity + rank
    source = jnp.full((slots,), -1, jnp.int32).at[slot].set(jnp.arange(per_event, dtype=jnp.int32))
    filled = source >= 0
    picked = jnp.maximum(source, 0)
    tags = jnp.where(filled, (local_user * span + offsets)[picked], -1).reshape(groups, capacity)
    both_weights = jnp.concatenate([w_key, w_value], axis=1)
    raw = jnp.where(filled[:, None], events[picked], 0).reshape(groups, capacity, events.shape[1])
    rows = lax.all_to_all(raw, "user", split_axis=0, concat_axis=0, tiled=True)
    marks = lax.all_to_all(tags, "user", split_axis=0, concat_axis=0, tiled=True)
    made = jnp.einsum("gcf,fe->gce", rows, both_weights, preferred_element_type=jnp.float32)
    arrived = made.astype(jnp.bfloat16)
    arrived_tags = marks
    arrived = arrived.reshape(slots, 2 * width)
    marks = arrived_tags.reshape(slots)
    owner_here = marks // span
    offset_here = marks - owner_here * span
    base = lax.axis_index("pos") * block_rows
    pick_user = owner_here[:, None] == jnp.arange(users_here, dtype=jnp.int32)[None, :]
    hist_here = jnp.sum(jnp.where(pick_user, hist_len[None, :], 0), axis=1)
    place = hist_here + offset_here - base
    good = (marks >= 0) & (place >= 0) & (place < block_rows)
    flat = jnp.where(good, owner_here * block_rows + place, users_here * block_rows).astype(
        jnp.int32
    )
    mapping = (
        jnp.full((users_here * block_rows,), -1, jnp.int32)
        .at[flat]
        .set(jnp.arange(slots, dtype=jnp.int32), mode="drop")
    )
    written = mapping >= 0
    taken = arrived[jnp.maximum(mapping, 0)]
    new_keys = jnp.where(written[:, None], taken[:, :width], cache_keys.reshape(-1, width)).reshape(
        cache_keys.shape
    )
    new_values = jnp.where(
        written[:, None], taken[:, width:], cache_values.reshape(-1, width)
    ).reshape(cache_values.shape)
    queries = lax.all_gather(candidates, "pos", axis=1, tiled=True)
    position = base + jnp.arange(block_rows, dtype=jnp.int32)
    valid_all = (position[None, :] < hist_len[:, None]) | written.reshape(users_here, block_rows)
    scale = width ** (-0.5)
    maxima = []
    sums = []
    partial_rows = []
    for user in range(users_here):
        scores = (
            jnp.einsum(
                "cd,pd->cp", queries[user], new_keys[user], preferred_element_type=jnp.float32
            )
            * scale
        )
        valid = valid_all[user][None, :]
        masked = jnp.where(valid, scores, jnp.float32(-1e30))
        block_max = jnp.max(masked, axis=1)
        expo = jnp.where(valid, jnp.exp(masked - block_max[:, None]), jnp.float32(0.0))
        sums.append(jnp.sum(expo, axis=1))
        maxima.append(block_max)
        weights = expo.astype(jnp.bfloat16)
        partial_rows.append(jnp.dot(weights, new_values[user], preferred_element_type=jnp.float32))
    block_max = jnp.stack(maxima)
    block_sum = jnp.stack(sums)
    parts = jnp.stack(partial_rows)
    count_q = candidates.shape[1]
    top, total, acc = joined((block_max, block_sum, parts), "pos", join_partials)
    start = lax.axis_index("pos") * count_q
    total = lax.dynamic_slice_in_dim(total, start, count_q, 1)
    acc = lax.dynamic_slice_in_dim(acc, start, count_q, 1)
    flag = active.astype(jnp.float32)[:, None, None]
    attended = (acc / total[..., None] * flag).astype(jnp.bfloat16)
    return (new_keys, new_values, attended)


def solution(mesh):
    placed = (
        P("user", None),
        P("user"),
        P("user"),
        P(),
        P(),
        P("user", "pos", None),
        P("user", "pos", None),
        P("user"),
        P("user"),
        P("user", "pos", None),
    )
    return jax.shard_map(
        on_device,
        mesh=mesh,
        in_specs=placed,
        out_specs=(P("user", "pos", None), P("user", "pos", None), P("user", "pos", None)),
        check_vma=False,
    )
```

profile of v0, /device:TPU:1, one launch (start us, length us, event | category | flops | bytes accessed | tf_op | source)
XLA Modules:
  0.0 178.3 jit_solution(950826465210066533)
XLA Ops:
  7.2 0.8 add_select_fusion.1
  7.9 2.3 %reduce-window.6 = s32[8,8,128]{2,1,0:T(8,128)S(1)} reduce-window(s32[8,8,128]{2,1,0:T(8,128)S(1)} %fusion.31, s32[]{:T(128)} %constant.107.clone.1), window={size=1x1x128 pad=0_0x0_0x127_0}, to_apply=%region_0.1 | reduce-window | flops 1040384 | bytes 65540 | tf_op jit(solution)/shard_map/reduce-window
  10.8 0.7 multiply_add_fusion
  11.5 4.3 %scatter_custom_fusion = s32[2048]{0:T(1024)S(1)} fusion(s32[1024]{0:T(1024)S(1)} %get-tuple-element.207, s32[1024]{0:T(1024)S(1)} %iota.23, s32[]{:T(128)} %constant.105.clone.1), kind=kCustom, calls=%fused_computation.87 | custom fusion | bytes 8196 | tf_op jit(solution)/shard_map/scatter | solution.py:44
  15.8 8.6 %gather_fusion = s32[2048]{0:T(1024)S(1)} fusion(s32[1024]{0:T(1024)S(1)} %get-tuple-element.206, s32[2048]{0:T(1024)S(1)} %maximum_clamp_fusion.1), kind=kCustom, calls=%fused_computation | custom fusion | bytes 24576 | tf_op jit(solution)/shard_map/gather | solution.py:47
  25.0 6.3 %all-to-all-start = ((s32[8,1,256]{2,1,0:T(1,128)}), s32[8,1,256]{2,1,0:T(1,128)S(1)}, u32[]{:S(2)}, u32[]{:S(2)}) async-start(s32[8,1,256]{2,1,0:T(1,128)} %bitcast.5), calls=%async_computation | async-start | bytes 16384 | tf_op jit(solution)/shard_map/all_to_all | solution.py:51
  31.4 0.7 all-gather.8.cloned.1.call-update
  32.1 7.5 %gather_fusion.1 = bf16[2048,256]{1,0:T(8,128)(2,1)S(1)} fusion(bf16[1024,256]{1,0:T(8,128)(2,1)S(1)} %copy-done, s32[2048]{0:T(1024)S(1)} %maximum_clamp_fusion.1), kind=kCustom, calls=%fused_computation.1 | custom fusion | bytes 2105344 | tf_op jit(solution)/shard_map/gather | solution.py:49
  39.7 1.2 broadcast_select_fusion
  40.9 5.4 %all-to-all-start.1 = ((bf16[8,256,256]{2,1,0:T(8,128)(2,1)}), bf16[8,256,256]{2,1,0:T(8,128)(2,1)}, u32[]{:S(2)}, u32[]{:S(2)}) async-start(bf16[8,256,256]{2,1,0:T(8,128)(2,1)} %broadcast_select_fusion), calls=%async_computation.1 | async-start | bytes 2097152 | tf_op jit(solution)/shard_map/all_to_all | solution.py:50
  46.7 8.2 %scatter_custom_fusion.1 = s32[3072]{0:T(1024)S(1)} fusion(s32[2048]{0:T(1024)S(1)} %bitcast.98, s32[2048]{0:T(1024)S(1)} %iota.24, s32[]{:T(128)} %constant.105.clone.1), kind=kCustom, calls=%fused_computation.80 | custom fusion | bytes 12292 | tf_op jit(solution)/shard_map/scatter | solution.py:70
  55.1 15.9 %all-to-all-done.1 = bf16[8,256,256]{2,1,0:T(8,128)(2,1)} async-done(((bf16[8,256,256]{2,1,0:T(8,128)(2,1)}), bf16[8,256,256]{2,1,0:T(8,128)(2,1)}, u32[]{:S(2)}, u32[]{:S(2)}) %all-to-all-start.1) | async-done | bytes 1048608 | tf_op jit(solution)/shard_map/all_to_all | solution.py:50
  71.0 1.9 %convolution_convert_fusion = bf16[8,256,512]{2,1,0:T(8,128)(2,1)S(1)} fusion(bf16[8,256,256]{2,1,0:T(8,128)(2,1)} %all-to-all-done.1, bf16[256,256]{1,0:T(8,128)(2,1)S(1)} %copy-done.5, bf16[256,256]{1,0:T(8,128)(2,1)S(1)} %copy-done.6), kind=kOutput, calls=%fused_computation.28 | convolution fusion | flops 538443776 | bytes 3407872 | tf_op jit(solution)/shard_map/gcf,fe->gce/dot_general | solution.py:52
  72.9 13.2 %gather_fusion.2 = bf16[3072,512]{1,0:T(8,128)(2,1)} fusion(bf16[2048,512]{1,0:T(8,128)(2,1)S(1)} %bitcast.85, s32[3072]{0:T(1024)S(1)} %maximum_clamp_fusion), kind=kCustom, calls=%fused_computation.2 | custom fusion | bytes 6303744 | tf_op jit(solution)/shard_map/gather | solution.py:73
  86.1 4.5 %slice_select_fusion = (bf16[3072,256]{1,0:T(8,128)(2,1)S(1)}, bf16[3072,256]{1,0:T(8,128)(2,1)}) fusion(bf16[3072,512]{1,0:T(8,128)(2,1)} %gather_fusion.2, bf16[2,1536,256]{2,1,0:T(8,128)(2,1)} %param.18, pred[3072]{0:T(1024)(128)(4,1)S(1)} %broadcast_compare_fusion, bf16[2,1536,256]{2,1,0:T(8,128)(2,1)} %param.17), kind=kLoop, calls=%fused_computation.29 | loop fusion | flops 1572864 | bytes 9440256 | tf_op jit(solution)/shard_map/jit(_where)/select_n | solution.py:77
  90.6 3.2 %fusion.4 = (f32[1024]{0:T(1024)S(1)}, f32[1536,1024]{1,0:T(8,128)S(1)}) fusion(pred[1536]{0:T(1024)(128)(4,1)S(1)} %get-tuple-element.183, bf16[2,1024,256]{2,1,0:T(8,128)(2,1)} %all-gather.8.cloned.1.call-done, bf16[3072,256]{1,0:T(8,128)(2,1)} %get-tuple-element.205), kind=kOutput, calls=%fused_computation.18 | convolution fusion | flops 810023936 | bytes 7607808 | tf_op jit(solution)/shard_map/cd,pd->cp/dot_general | solution.py:89
  93.9 2.0 %fusion.18 = f32[1,1024,256]{2,1,0:T(8,128)S(1)} fusion(f32[1536,1024]{1,0:T(8,128)S(1)} %get-tuple-element.211, f32[1024]{0:T(1024)S(1)} %get-tuple-element.210, pred[1536]{0:T(1024)(128)(4,1)S(1)} %get-tuple-element.183, bf16[3072,256]{1,0:T(8,128)(2,1)S(1)} %get-tuple-element.204), kind=kOutput, calls=%fused_computation.32 | convolution fusion | flops 813170688 | bytes 8132608 | tf_op jit(solution)/shard_map/dot_general | solution.py:101
  95.9 1.0 copy-done.1
  96.9 0.6 copy-done.8
  97.5 1.0 fusion.3
  98.6 2.0 %fusion.15 = f32[1,1024,256]{2,1,0:T(8,128)S(1)} fusion(f32[1536,1024]{1,0:T(8,128)S(1)} %get-tuple-element.213, f32[1024]{0:T(1024)S(1)} %get-tuple-element.212, pred[1536]{0:T(1024)(128)(4,1)S(1)} %get-tuple-element.182, bf16[3072,256]{1,0:T(8,128)(2,1)S(1)} %get-tuple-element.204), kind=kOutput, calls=%fused_computation.31 | convolution fusion | flops 813170688 | bytes 8132608 | tf_op jit(solution)/shard_map/dot_general | solution.py:101
  101.2 1.5 pad_maximum_fusion
  102.7 7.4 %all-gather.3 = f32[4,2,1024]{2,1,0:T(2,128)S(1)} all-gather(f32[1,2,1024]{2,1,0:T(2,128)S(1)} %maximum_bitcast_fusion.2), channel_id=2, replica_groups=mesh['user'=8,'pos'=4] {'pos'}, dimensions={0}, use_global_device_ids=true | all-gather | bytes 40960 | tf_op jit(solution)/shard_map/all_gather | solution.py:8
  110.1 8.5 %fusion.5 = (f32[1024]{0:T(1024)S(1)}, f32[1024]{0:T(1024)S(1)}) fusion(f32[1536,1024]{1,0:T(8,128)} %copy-done.2, f32[1024]{0:T(1024)S(1)} %get-tuple-element.212, pred[1536]{0:T(1024)(128)(4,1)S(1)} %get-tuple-element.182, f32[1024]{0:T(1024)S(1)} %get-tuple-element.210, f32[1536,1024]{1,0:T(8,128)} %copy-done.1, pred[1536]{0:T(1024)(128)(4,1)S(1)} %get-tuple-element.183), kind=kLoop, calls=%fused_computation.19 | loop fusion | flops 15726592 | bytes 12602368 | tf_op jit(solution)/shard_map/reduce_sum | solution.py:98
  118.6 5.5 %all-gather.4 = f32[4,2,1024]{2,1,0:T(2,128)S(1)} all-gather(f32[1,2,1024]{2,1,0:T(2,128)S(1)} %maximum_bitcast_fusion.3), channel_id=3, replica_groups=mesh['user'=8,'pos'=4] {'pos'}, dimensions={0}, use_global_device_ids=true | all-gather | bytes 40960 | tf_op jit(solution)/shard_map/all_gather | solution.py:8
  124.1 38.1 %all-gather.10.cloned.1.call-done = f32[8,1024,256]{2,1,0:T(8,128)} async-done(((f32[2,1024,256]{2,1,0:T(8,128)}), f32[8,1024,256]{2,1,0:T(8,128)}) %all-gather.10.cloned.1.call-update) | async-done | bytes 8388624 | tf_op jit(solution)/shard_map/all_gather | solution.py:8
  162.2 1.7 slice.79
  163.9 6.7 %while.19 = (s32[]{:T(128)}, f32[2,1024]{1,0:T(2,128)S(1)}, f32[2,1024]{1,0:T(2,128)S(1)}, f32[2,1024,256]{2,1,0:T(8,128)S(1)}, f32[4,2,1024]{2,1,0:T(2,128)S(1)...) while((s32[]{:T(128)}, f32[2,1024]{1,0:T(2,128)S(1)}, ...), condition=%wide.region_11.12_spmd, body=%wide.region_10.11_spmd.sunk | while | flops 1585157 | bytes 6373527 | solution.py:13
  164.0 2.2 %fusion.53 = f32[2,1024,256]{2,1,0:T(8,128)S(1)} fusion(f32[4,2,1024,256]{3,2,1,0:T(8,128)} %get-tuple-element.293, s32[]{:T(128)S(6)} %select_n.188, f32[2,1024,256]{2,1,0:T(8,128)S(1)} %get-tuple-element.280, f32[2,1024]{1,0:T(2,128)S(1)} %get-tuple-element.265, f32[2,1024]{1,0:T(2,128)S(1)} %get-tuple-element.266), kind=kLoop, calls=%fused_computation.6.clone.1 | loop fusion | flops 1572864 | bytes 6307844 | tf_op jit(solution)/shard_map/while/body/eval_jaxpr/add | solution.py:23
  166.2 2.2 %fusion.53 = f32[2,1024,256]{2,1,0:T(8,128)S(1)} fusion(f32[4,2,1024,256]{3,2,1,0:T(8,128)} %get-tuple-element.293, s32[]{:T(128)S(6)} %select_n.188, f32[2,1024,256]{2,1,0:T(8,128)S(1)} %get-tuple-element.280, f32[2,1024]{1,0:T(2,128)S(1)} %get-tuple-element.265, f32[2,1024]{1,0:T(2,128)S(1)} %get-tuple-element.266), kind=kLoop, calls=%fused_computation.6.clone.1 | loop fusion | flops 1572864 | bytes 6307844 | tf_op jit(solution)/shard_map/while/body/eval_jaxpr/add | solution.py:23
  168.4 2.2 %fusion.53 = f32[2,1024,256]{2,1,0:T(8,128)S(1)} fusion(f32[4,2,1024,256]{3,2,1,0:T(8,128)} %get-tuple-element.293, s32[]{:T(128)S(6)} %select_n.188, f32[2,1024,256]{2,1,0:T(8,128)S(1)} %get-tuple-element.280, f32[2,1024]{1,0:T(2,128)S(1)} %get-tuple-element.265, f32[2,1024]{1,0:T(2,128)S(1)} %get-tuple-element.266), kind=kLoop, calls=%fused_computation.6.clone.1 | loop fusion | flops 1572864 | bytes 6307844 | tf_op jit(solution)/shard_map/while/body/eval_jaxpr/add | solution.py:23
  170.6 0.9 multiply_convert_fusion
  (55 shorter events, 2.4 us)
Async XLA Ops:
  7.2 24.9 %copy-start = (bf16[1024,256]{1,0:T(8,128)(2,1)S(1)}, bf16[1024,256]{1,0:T(8,128)(2,1)}, u32[]{:S(2)}) copy-start(bf16[1024,256]{1,0:T(8,128)(2,1)} %param.12) | copy-start | bytes 1572868
  25.0 15.9 %all-to-all-start = ((s32[8,1,256]{2,1,0:T(1,128)}), s32[8,1,256]{2,1,0:T(1,128)S(1)}, u32[]{:S(2)}, u32[]{:S(2)}) async-start(s32[8,1,256]{2,1,0:T(1,128)} %bitcast.5), calls=%async_computation | async-start | bytes 16384 | tf_op jit(solution)/shard_map/all_to_all | solution.py:51
  31.4 59.2 %all-gather.8.cloned.1.call-start = ((), (), s32[]{:S(2)}) async-start(), calls=%async_computation.2 | async-start | bytes 1310720 | tf_op jit(solution)/shard_map/all_gather | solution.py:80
  39.6 6.8 %copy-start.7 = (s32[2]{0:T(128)S(1)}, s32[2]{0:T(128)}, u32[]{:S(2)}) copy-start(s32[2]{0:T(128)} %param.19) | copy-start | bytes 28
  39.6 31.4 %copy-start.5 = (bf16[256,256]{1,0:T(8,128)(2,1)S(1)}, bf16[256,256]{1,0:T(8,128)(2,1)}, u32[]{:S(2)}) copy-start(bf16[256,256]{1,0:T(8,128)(2,1)} %param.16) | copy-start | bytes 393220
  39.6 31.4 %copy-start.6 = (bf16[256,256]{1,0:T(8,128)(2,1)S(1)}, bf16[256,256]{1,0:T(8,128)(2,1)}, u32[]{:S(2)}) copy-start(bf16[256,256]{1,0:T(8,128)(2,1)} %param.15) | copy-start | bytes 393220
  40.9 30.1 %all-to-all-start.1 = ((bf16[8,256,256]{2,1,0:T(8,128)(2,1)}), bf16[8,256,256]{2,1,0:T(8,128)(2,1)}, u32[]{:S(2)}, u32[]{:S(2)}) async-start(bf16[8,256,256]{2,1,0:T(8,128)(2,1)} %broadcast_select_fusion), calls=%async_computation.1 | async-start | bytes 2097152 | tf_op jit(solution)/shard_map/all_to_all | solution.py:50
  46.4 115.8 %all-gather.10.cloned.1.call-start = ((), (), s32[]{:S(2)}) async-start(), calls=%async_computation.3 | async-start | bytes 10485760 | tf_op jit(solution)/shard_map/all_gather | solution.py:8
  90.6 8.0 %copy-start.3 = (bf16[3072,256]{1,0:T(8,128)(2,1)}, bf16[3072,256]{1,0:T(8,128)(2,1)S(1)}, u32[]{:S(2)}) copy-start(bf16[3072,256]{1,0:T(8,128)(2,1)S(1)} %get-tuple-element.204) | copy-start | bytes 4718596
  93.9 3.0 %copy-start.1 = (f32[1536,1024]{1,0:T(8,128)}, f32[1536,1024]{1,0:T(8,128)S(1)}, u32[]{:S(2)}) copy-start(f32[1536,1024]{1,0:T(8,128)S(1)} %get-tuple-element.211) | copy-start | bytes 18874372
  93.9 3.0 %copy-start.4 = (bf16[3072,256]{1,0:T(8,128)(2,1)S(1)}, bf16[3072,256]{1,0:T(8,128)(2,1)}, u32[]{:S(2)}) copy-start(bf16[3072,256]{1,0:T(8,128)(2,1)} %get-tuple-element.205) | copy-start | bytes 4718596
  93.9 3.7 %copy-start.8 = (bf16[2,1024,256]{2,1,0:T(8,128)(2,1)S(1)}, bf16[2,1024,256]{2,1,0:T(8,128)(2,1)}, u32[]{:S(2)}) copy-start(bf16[2,1024,256]{2,1,0:T(8,128)(2,1)} %all-gather.8.cloned.1.call-done) | copy-start | bytes 3145732
  98.6 2.6 %copy-start.2 = (f32[1536,1024]{1,0:T(8,128)}, f32[1536,1024]{1,0:T(8,128)S(1)}, u32[]{:S(2)}) copy-start(f32[1536,1024]{1,0:T(8,128)S(1)} %get-tuple-element.213) | copy-start | bytes 18874372
  101.2 1.5 copy-start.9
Sparse Core Ops, SparseCore 0:
  33.7 18.7 all-gather.7
  102.8 59.3 all-gather.9
where the time goes:
time: 179 us; the launch traced here: 178 us
  waiting for transfers between devices  54.7 us (31%)
  local copies, waits for them, and re-layouts  46.1 us (26%)
  other arithmetic  28 us (16%)
  between operations  14.4 us (8%)
  blocking collectives  12.9 us (7%)
  starting transfers between devices  11.8 us (7%)
  matrix products  10.3 us (6%)
    all_gather x1, waiting for transfers between devices, joined(): gathered = jax.tree.map(lambda a: lax.all_gather(a, axis), part)  38.1 us
    all_to_all x1, waiting for transfers between devices, on_device(): rows = lax.all_to_all(raw, 'user', split_axis=0, concat_axis=0, tiled=True)  15.9 us
    gather x1, local copies, waits for them, and re-layouts, on_device(): taken = arrived[jnp.maximum(mapping, 0)]  13.2 us
    all_gather x2, blocking collectives, joined(): gathered = jax.tree.map(lambda a: lax.all_gather(a, axis), part)  12.9 us
    gather x1, local copies, waits for them, and re-layouts, on_device(): (local_user * span + offsets)[picked]  8.58 us
    reduce_sum x1, other arithmetic, on_device(): sums.append(jnp.sum(expo, axis=1))  8.48 us
    scatter x1, local copies, waits for them, and re-layouts, on_device(): mapping = jnp.full((users_here * block_rows,), -1, jnp.int32).at[flat].se...  8.24 us
    gather x1, local copies, waits for them, and re-layouts, on_device(): events[picked]  7.5 us
  transfers between devices with their start and end apart: 4, of which 2 were waited for; matrix products, arithmetic and copies ran while one was open for 25% of the time, Pallas kernels for 0%

commit v1 on v0

v1 whole, which is shorter than its diff:
```python
import functools
import math

import jax
import jax.numpy as jnp
from jax import lax
from jax.experimental import pallas as pl
from jax.experimental.pallas import tpu as pltpu
from jax.sharding import PartitionSpec as P

MESH = pl.DeviceIdType.MESH
NT = (((1,), (1,)), ((), ()))
TAIL = 16


def pos_peers():
    p = lax.axis_index("pos")
    near = p + 1 - 2 * lax.rem(p, 2)
    far = lax.rem(p + 2, 4)
    return p, near, far


def exchange_kernel(
    groups, blocks, users_here, cap,
    events_ref, owners_ref, cand_ref,
    rows_ref, queries_ref,
    packed, local_sem, a2a_send, a2a_recv, hop_send, hop_recv, q_send, q_recv,
):
    me = lax.axis_index("user")
    p, near, far = pos_peers()
    count = groups // blocks
    first = lax.rem(p - me + blocks * groups, blocks)
    far_first = lax.rem(far - me + blocks * groups, blocks)
    peers = [first + blocks * k for k in range(count)]

    barrier = pltpu.get_barrier_semaphore()
    for peer in (near, far):
        pl.semaphore_signal(barrier, inc=1, device_id={"pos": peer}, device_id_type=MESH)
    for peer in peers:
        @pl.when(peer != me)
        def _():
            pl.semaphore_signal(barrier, inc=1, device_id={"user": peer}, device_id_type=MESH)
    itself = (lax.rem(me, blocks) == first).astype(jnp.int32)
    pl.semaphore_wait(barrier, 2 + count - itself)

    def hop(ref_src, ref_dst, send, recv, peer):
        return pltpu.make_async_remote_copy(
            src_ref=ref_src, dst_ref=ref_dst, send_sem=send, recv_sem=recv,
            device_id={"pos": peer}, device_id_type=MESH,
        )

    q_far = hop(cand_ref, queries_ref.at[p], q_send.at[0], q_recv.at[0], far)
    q_far.start()
    q_near = hop(cand_ref, queries_ref.at[p], q_send.at[1], q_recv.at[1], near)
    q_near.start()
    q_own = pltpu.make_async_copy(cand_ref, queries_ref.at[p], local_sem.at[count])
    q_own.start()

    per_event = events_ref.shape[0]
    width = events_ref.shape[1]
    users = groups * users_here
    owner = owners_ref[...]
    user_id = lax.broadcasted_iota(jnp.int32, (users, per_event), 0)
    same = (user_id == owner).astype(jnp.float32)
    before = (
        lax.broadcasted_iota(jnp.int32, (per_event, per_event), 0)
        <= lax.broadcasted_iota(jnp.int32, (per_event, per_event), 1)
    ).astype(jnp.float32).astype(jnp.bfloat16)
    ranks = jnp.dot(same.astype(jnp.bfloat16), before, preferred_element_type=jnp.float32)
    counts = jnp.sum(same, axis=1, keepdims=True)
    dest = owner // users_here
    earlier = (user_id >= dest * users_here) & (user_id < owner)
    slot = jnp.sum(jnp.where(earlier, counts, 0.0) + same * ranks, axis=0, keepdims=True) - 1.0
    slot = slot.astype(jnp.int32)
    slot_id = lax.broadcasted_iota(jnp.int32, (cap, per_event), 0)
    lane = lax.broadcasted_iota(jnp.int32, (users, width), 1)
    lane_user = lax.broadcasted_iota(jnp.int32, (users, width), 0)

    def a2a(k, peer, slot):
        return pltpu.make_async_remote_copy(
            src_ref=packed.at[k], dst_ref=rows_ref.at[me],
            send_sem=a2a_send.at[k], recv_sem=a2a_recv.at[slot],
            device_id={"user": peer}, device_id_type=MESH,
        )

    def own(k):
        return pltpu.make_async_copy(packed.at[k], rows_ref.at[me], local_sem.at[k])

    for k, peer in enumerate(peers):
        wanted = jnp.where(dest == peer, slot, -1)
        pick = (wanted == slot_id).astype(jnp.float32).astype(jnp.bfloat16)
        packed[k, :cap, :] = jnp.dot(
            pick, events_ref[...], preferred_element_type=jnp.float32
        ).astype(jnp.bfloat16)
        row = jnp.sum(
            jnp.where(lane_user == lane + peer * users_here, counts, 0.0), axis=0, keepdims=True
        )
        packed[k, cap:, :] = jnp.broadcast_to(row, (TAIL, width)).astype(jnp.bfloat16)

        @pl.when(peer != me)
        def _():
            a2a(k, peer, me // blocks).start()

        @pl.when(peer == me)
        def _():
            own(k).start()

    def forward(stage, k, start, peer):
        block = rows_ref.at[start + blocks * k]
        return hop(block, block, hop_send.at[stage, k], hop_recv.at[stage, k], peer)

    q_far.wait_recv()
    q_across = hop(queries_ref.at[far], queries_ref.at[far], q_send.at[2], q_recv.at[2], near)
    q_across.start()
    for k, peer in enumerate(peers):
        @pl.when(peer != me)
        def _():
            a2a(k, peer, k).wait_recv()

        @pl.when(peer == me)
        def _():
            own(k).wait()

        forward(0, k, first, far).start()
        forward(1, k, first, near).start()
    for k in range(count):
        forward(0, k, first, far).wait_recv()
        forward(2, k, far_first, near).start()
    for k in range(count):
        forward(1, k, first, near).wait_recv()
        forward(2, k, far_first, near).wait_recv()
    q_near.wait_recv()
    q_across.wait_recv()
    q_own.wait()
    q_far.wait_send()
    q_near.wait_send()
    q_across.wait_send()
    for k, peer in enumerate(peers):
        @pl.when(peer != me)
        def _():
            a2a(k, peer, k).wait_send()

        forward(0, k, first, far).wait_send()
        forward(1, k, first, near).wait_send()
        forward(2, k, far_first, near).wait_send()


def attend_kernel(
    groups, cap, scale,
    count_ref, hist_ref, rows_ref, weight_ref, keys_ref, values_ref, queries_ref,
    new_keys_ref, new_values_ref, part_ref, stat_ref,
    made, fresh, acc, top, total, eye,
):
    user = pl.program_id(0)
    step = pl.program_id(1)
    steps = pl.num_programs(1)
    rows = keys_ref.shape[1]
    width = keys_ref.shape[2]
    quarters, quarter = queries_ref.shape[0], queries_ref.shape[2]
    users_here = hist_ref.shape[0]

    @pl.when((user == 0) & (step == 0))
    def _():
        def project(g, carry):
            made[g] = jnp.dot(
                rows_ref[g, :cap, :], weight_ref[...], preferred_element_type=jnp.float32
            ).astype(jnp.bfloat16)
            return carry

        lax.fori_loop(0, groups, project, 0)
        eye[...] = (
            lax.broadcasted_iota(jnp.int32, (width, width), 0)
            == lax.broadcasted_iota(jnp.int32, (width, width), 1)
        ).astype(jnp.float32).astype(jnp.bfloat16)

    @pl.when(step == 0)
    def _():
        acc[...] = jnp.zeros_like(acc)
        top[...] = jnp.full_like(top, -1e30)
        total[...] = jnp.zeros_like(total)

    origin = (lax.axis_index("pos") * steps + step) * rows
    start = hist_ref[user] - origin
    limit = lax.fori_loop(0, groups, lambda g, n: n + count_ref[g, user], start)
    touched = (limit > 0) & (start < rows) & (limit > start)
    new_keys_ref[...] = keys_ref[...]
    new_values_ref[...] = values_ref[...]

    @pl.when(touched)
    def _():
        fresh[...] = jnp.zeros_like(fresh)
        gap = lax.broadcasted_iota(jnp.int32, (rows, cap), 1) - lax.broadcasted_iota(
            jnp.int32, (rows, cap), 0
        )
        slot = lax.broadcasted_iota(jnp.int32, (rows, cap), 1)

        def place(g, at):
            size = count_ref[g, user]

            @pl.when((size > 0) & (at < rows) & (at + size > 0))
            def _():
                low = lax.fori_loop(0, user, lambda j, n: n + count_ref[g, j], 0)
                pick = (gap == low - at) & (slot >= low) & (slot < low + size)
                fresh[...] += jnp.dot(
                    pick.astype(jnp.float32).astype(jnp.bfloat16), made[g],
                    preferred_element_type=jnp.float32,
                )

            return at + size

        lax.fori_loop(0, groups, place, start)
        row = lax.broadcasted_iota(jnp.int32, (rows, width), 0)
        inside = (row >= start) & (row < limit)
        new_keys_ref[0] = jnp.where(
            inside, fresh[:, :width], keys_ref[0].astype(jnp.float32)
        ).astype(jnp.bfloat16)
        new_values_ref[0] = jnp.where(
            inside, fresh[:, width:], values_ref[0].astype(jnp.float32)
        ).astype(jnp.bfloat16)

    @pl.when(limit > 0)
    def _():
        keys = new_keys_ref[0]
        flipped = lax.dot_general(
            eye[...], new_values_ref[0], NT, preferred_element_type=jnp.float32
        ).astype(jnp.bfloat16)
        valid = lax.broadcasted_iota(jnp.int32, (rows, quarter), 0) < limit
        for c in range(quarters):
            scores = lax.dot_general(
                keys, queries_ref[c, 0], NT, preferred_element_type=jnp.float32
            ) * (scale * math.log2(math.e))
            scores = jnp.where(valid, scores, -1e30)
            old = top[c : c + 1]
            high = jnp.maximum(old, jnp.max(scores, axis=0, keepdims=True))
            expo = jnp.exp2(scores - high)
            shrink = jnp.exp2(old - high)
            top[c : c + 1] = high
            total[c : c + 1] = total[c : c + 1] * shrink + jnp.sum(expo, axis=0, keepdims=True)
            acc[c] = acc[c] * shrink + jnp.dot(
                flipped, expo.astype(jnp.bfloat16), preferred_element_type=jnp.float32
            )

    @pl.when(step == steps - 1)
    def _():
        part_ref[:, 0] = acc[...].astype(jnp.bfloat16)
        for c in range(quarters):
            stat_ref[c, 0] = jnp.concatenate(
                [
                    jnp.broadcast_to(top[c : c + 1], (4, quarter)),
                    jnp.broadcast_to(total[c : c + 1], (4, quarter)),
                ],
                axis=0,
            )


def combine_kernel(
    part_ref, stat_ref, active_ref, out_ref,
    near_part, near_stat, send_part, send_stat, far_part, far_stat,
    near_send, near_recv, far_send, far_recv,
):
    p, near, far = pos_peers()
    low = lax.rem(p, 2)
    high = p // 2
    users_here = part_ref.shape[1]
    barrier = pltpu.get_barrier_semaphore()
    for peer in (near, far):
        pl.semaphore_signal(barrier, inc=1, device_id={"pos": peer}, device_id_type=MESH)
    pl.semaphore_wait(barrier, 2)

    def copies(src_part, src_stat, dst_part, dst_stat, send, recv, n, peer):
        return [
            pltpu.make_async_remote_copy(
                src_ref=src, dst_ref=dst, send_sem=send.at[i, n], recv_sem=recv.at[i, n],
                device_id={"pos": peer}, device_id_type=MESH,
            )
            for i, (src, dst) in enumerate(((src_part, dst_part), (src_stat, dst_stat)))
        ]

    theirs = (2 * (1 - high) + low, p)
    first = {}
    for h, quarter in enumerate((2 * (1 - high) + 1 - low, near)):
        for u in range(users_here):
            first[h, u] = copies(
                part_ref.at[quarter, u], stat_ref.at[quarter, u],
                near_part.at[h, u], near_stat.at[h, u],
                near_send, near_recv, h * users_here + u, near,
            )
            for copy in first[h, u]:
                copy.start()

    def merge(a_stat, a_part, b_stat, b_part):
        a_top, b_top = a_stat[0:1], b_stat[0:1]
        top = jnp.maximum(a_top, b_top)
        a_factor = jnp.exp2(a_top - top)
        b_factor = jnp.exp2(b_top - top)
        total = a_stat[4:5] * a_factor + b_stat[4:5] * b_factor
        part = a_part.astype(jnp.float32) * a_factor + b_part.astype(jnp.float32) * b_factor
        return top, total, part

    def local(h, u):
        for copy in first[h, u]:
            copy.wait_recv()
        return merge(
            stat_ref[theirs[h], u], part_ref[theirs[h], u], near_stat[h, u], near_part[h, u]
        )

    second = []
    for u in range(users_here):
        top, total, part = local(0, u)
        send_part[u] = part.astype(jnp.bfloat16)
        send_stat[u] = jnp.concatenate(
            [jnp.broadcast_to(top, (4,) + top.shape[1:]), jnp.broadcast_to(total, (4,) + top.shape[1:])],
            axis=0,
        )
        second.append(
            copies(
                send_part.at[u], send_stat.at[u], far_part.at[u], far_stat.at[u],
                far_send, far_recv, u, far,
            )
        )
        for copy in second[u]:
            copy.start()
    kept = [local(1, u) for u in range(users_here)]
    for u in range(users_here):
        top, total, part = kept[u]
        for copy in second[u]:
            copy.wait_recv()
        other = far_stat[u]
        new_top = jnp.maximum(top, other[0:1])
        mine = jnp.exp2(top - new_top)
        theirs_factor = jnp.exp2(other[0:1] - new_top)
        total = total * mine + other[4:5] * theirs_factor
        flag = active_ref[u].astype(jnp.float32)
        inverse = flag / total
        whole = part * (mine * inverse) + far_part[u].astype(jnp.float32) * (theirs_factor * inverse)
        out_ref[u] = whole.T.astype(jnp.bfloat16)
    for group in list(first.values()) + second:
        for copy in group:
            copy.wait_send()


def on_device(
    events, owners, offsets, w_key, w_value, cache_keys, cache_values, hist_len, active, candidates
):
    groups = lax.axis_size("user")
    blocks = lax.axis_size("pos")
    users_here, block_rows, width = cache_keys.shape
    per_event, features = events.shape
    cap = 2 * per_event // groups
    quarter = candidates.shape[1]
    count = groups // blocks
    vmem = pl.BlockSpec(memory_space=pltpu.VMEM)
    smem = pl.BlockSpec(memory_space=pltpu.SMEM)
    dma = pltpu.SemaphoreType.DMA
    bf16, f32 = jnp.bfloat16, jnp.float32

    rows, queries = pl.pallas_call(
        functools.partial(exchange_kernel, groups, blocks, users_here, cap),
        out_shape=(
            jax.ShapeDtypeStruct((groups, cap + TAIL, features), bf16),
            jax.ShapeDtypeStruct((blocks, users_here, quarter, width), bf16),
        ),
        in_specs=[vmem] * 3,
        out_specs=(vmem, vmem),
        scratch_shapes=[
            pltpu.VMEM((count, cap + TAIL, features), bf16),
            dma((count + 1,)), dma((count,)), dma((count,)),
            dma((3, count)), dma((3, count)), dma((3,)), dma((3,)),
        ],
        compiler_params=pltpu.CompilerParams(collective_id=0, has_side_effects=True),
        name="exchange",
    )(events, owners.reshape(1, per_event), candidates)

    counts = rows[:, cap, :users_here].astype(jnp.int32)
    weights = jnp.concatenate([w_key, w_value], axis=1)
    step_rows = block_rows // 3
    cache_spec = pl.BlockSpec((1, step_rows, width), lambda u, b: (u, b, 0))
    new_keys, new_values, part, stat = pl.pallas_call(
        functools.partial(attend_kernel, groups, cap, width ** -0.5),
        grid=(users_here, block_rows // step_rows),
        out_shape=(
            jax.ShapeDtypeStruct(cache_keys.shape, bf16),
            jax.ShapeDtypeStruct(cache_values.shape, bf16),
            jax.ShapeDtypeStruct((blocks, users_here, width, quarter), bf16),
            jax.ShapeDtypeStruct((blocks, users_here, 8, quarter), f32),
        ),
        in_specs=[
            smem, smem, vmem, vmem, cache_spec, cache_spec,
            pl.BlockSpec((blocks, 1, quarter, width), lambda u, b: (0, u, 0, 0)),
        ],
        out_specs=(
            cache_spec, cache_spec,
            pl.BlockSpec((blocks, 1, width, quarter), lambda u, b: (0, u, 0, 0)),
            pl.BlockSpec((blocks, 1, 8, quarter), lambda u, b: (0, u, 0, 0)),
        ),
        scratch_shapes=[
            pltpu.VMEM((groups, cap, 2 * width), bf16),
            pltpu.VMEM((step_rows, 2 * width), f32),
            pltpu.VMEM((blocks, width, quarter), f32),
            pltpu.VMEM((blocks, quarter), f32),
            pltpu.VMEM((blocks, quarter), f32),
            pltpu.VMEM((width, width), bf16),
        ],
        compiler_params=pltpu.CompilerParams(
            dimension_semantics=("arbitrary", "arbitrary"), vmem_limit_bytes=40 * 2**20
        ),
        name="attend",
    )(counts, hist_len, rows, weights, cache_keys, cache_values, queries)

    attended = pl.pallas_call(
        combine_kernel,
        out_shape=jax.ShapeDtypeStruct(candidates.shape, bf16),
        in_specs=[vmem, vmem, smem],
        out_specs=vmem,
        scratch_shapes=[
            pltpu.VMEM((2, users_here, width, quarter), bf16),
            pltpu.VMEM((2, users_here, 8, quarter), f32),
            pltpu.VMEM((users_here, width, quarter), bf16),
            pltpu.VMEM((users_here, 8, quarter), f32),
            pltpu.VMEM((users_here, width, quarter), bf16),
            pltpu.VMEM((users_here, 8, quarter), f32),
            dma((2, 2 * users_here)), dma((2, 2 * users_here)),
            dma((2, users_here)), dma((2, users_here)),
        ],
        compiler_params=pltpu.CompilerParams(collective_id=1, has_side_effects=True),
        name="combine",
    )(part, stat, active)
    return (new_keys, new_values, attended)


def solution(mesh):
    placed = (
        P("user", None),
        P("user"),
        P("user"),
        P(),
        P(),
        P("user", "pos", None),
        P("user", "pos", None),
        P("user"),
        P("user"),
        P("user", "pos", None),
    )
    return jax.shard_map(
        on_device,
        mesh=mesh,
        in_specs=placed,
        out_specs=(P("user", "pos", None), P("user", "pos", None), P("user", "pos", None)),
        check_vma=False,
    )
```

time: 179 us -> 62.5 us (0.35)
  waiting for transfers between devices: 54.7 us -> 0 us
  Pallas kernels: 0 us -> 50.3 us
  local copies, waits for them, and re-layouts: 46.1 us -> 9.2 us
  other arithmetic: 28 us -> 1.71 us
  between operations: 14.4 us -> 0.66 us
  blocking collectives: 12.9 us -> 0 us
  starting transfers between devices: 11.8 us -> 0 us
  matrix products: 10.3 us -> 0 us
    pallas_call x0 -> x3, Pallas kernels: none -> 50.3 us  [the longest x1 23.4 us: on_device(): pl.pallas_call(functools.partial(exchange_kernel, groups, blocks, users_h...]
    all_gather x2 -> x0, waiting for transfers between devices: 38.1 us -> none  [the longest x1 38.1 us: joined(): gathered = jax.tree.map(lambda a: lax.all_gather(a, axis), part)]
    gather x3 -> x0, local copies, waits for them, and re-layouts: 29.3 us -> none  [the longest x1 13.2 us: on_device(): taken = arrived[jnp.maximum(mapping, 0)]]
    all_to_all x2 -> x0, waiting for transfers between devices: 15.9 us -> none  [the longest x1 15.9 us: on_device(): rows = lax.all_to_all(raw, 'user', split_axis=0, concat_axis=0, tiled=True)]
    all_gather x2 -> x0, blocking collectives: 12.9 us -> none  [joined(): gathered = jax.tree.map(lambda a: lax.all_gather(a, axis), part)]
    scatter x2 -> x0, local copies, waits for them, and re-layouts: 12.6 us -> none  [the longest x1 8.24 us: on_device(): mapping = jnp.full((users_here * block_rows,), -1, jnp.int32).at[flat].se...]
    all_to_all x2 -> x0, starting transfers between devices: 11.8 us -> none  [the longest x1 6.34 us: on_device(): lax.all_to_all(tags, 'user', split_axis=0, concat_axis=0, tiled=True)]
    dot_general x5 -> x0, matrix products: 10.3 us -> none  [the longest x2 4.29 us: on_device(): jnp.einsum('cd,pd->cp', queries[user], new_keys[user], preferred_element_...]
  transfers between devices with their start and end apart: 4 -> 0, of which waited for: 2 -> 0; matrix products, arithmetic and copies ran while one was open for 25% -> 0% of each run, Pallas kernels for 0% -> 0%
where the time goes in v1:
time: 62.5 us; the launch traced here: 61.9 us
  Pallas kernels  50.3 us (80%)
  local copies, waits for them, and re-layouts  9.2 us (15%)
  other arithmetic  1.71 us (3%)
  between operations  0.66 us (1%)
    pallas_call x1, Pallas kernels, on_device(): pl.pallas_call(functools.partial(exchange_kernel, groups, blocks, users_h...  23.4 us
    pallas_call x1, Pallas kernels, on_device(): pl.pallas_call(combine_kernel, out_shape=jax.ShapeDtypeStruct(candidates....  18 us
    unnamed x15, local copies, waits for them, and re-layouts  9.2 us
    pallas_call x1, Pallas kernels, on_device(): pl.pallas_call(functools.partial(attend_kernel, groups, cap, width ** (-0...  8.93 us

profile of v1, /device:TPU:1, one launch (start us, length us, event | category | flops | bytes accessed | tf_op | source)
XLA Modules:
  0.0 61.9 jit_solution(1253690675236917656)
XLA Ops:
  0.6 1.0 %pad_maximum_fusion.weight_ref = bf16[256,512]{1,0:T(8,128)(2,1)S(1)} fusion(bf16[256,256]{1,0:T(8,128)(2,1)} %param.13, bf16[256,256]{1,0:T(8,128)(2,1)} %param.12), kind=kLoop, calls=%fused_computation | loop fusion | flops 524288 | bytes 524288 | tf_op jit(solution)/shard_map/concatenate | solution.py:375
  1.6 23.4 %exchange.1 = (bf16[8,272,256]{2,1,0:T(8,128)(2,1)}, bf16[4,2,256,256]{3,2,1,0:T(8,128)(2,1)}) custom-call(bf16[1024,256]{1,0:T(8,128)(2,1)} %events_ref.1, s32[1,1024]{1,0:T(1,128)} %bitcast.3, bf16[2,256,256]{2,1,0:T(8,128)(2,1)} %cand_ref.1), custom_call_target="tpu_custom_call" | custom-call | tf_op jit(solution)/shard_map/exchange/pallas_call | solution.py:357
  25.0 0.7 %slice_convert_fusion = s32[8,1,2]{2,1,0:T(1,128)S(1)} fusion(bf16[8,272,256]{2,1,0:T(8,128)(2,1)} %get-tuple-element.9.rows_ref), kind=kLoop, calls=%fused_computation.1 | loop fusion | flops 16 | bytes 96 | tf_op jit(solution)/shard_map/convert_element_type | solution.py:374
  25.7 0.0 copy-start
  25.7 1.4 %copy-done = bf16[2,1536,256]{2,1,0:T(8,128)(2,1)S(1)} copy-done((bf16[2,1536,256]{2,1,0:T(8,128)(2,1)S(1)}, bf16[2,1536,256]{2,1,0:T(8,128)(2,1)}, u32[]{:S(2)}) %copy-start) | copy-done | bytes 1572888
  27.1 0.0 copy-start.1
  27.1 1.4 %copy-done.1 = bf16[2,1536,256]{2,1,0:T(8,128)(2,1)S(1)} copy-done((bf16[2,1536,256]{2,1,0:T(8,128)(2,1)S(1)}, bf16[2,1536,256]{2,1,0:T(8,128)(2,1)}, u32[]{:S(2)}) %copy-start.1) | copy-done | bytes 1572888
  28.5 0.0 copy-start.2
  28.5 1.2 %copy-done.2 = bf16[8,272,256]{2,1,0:T(8,128)(2,1)S(1)} copy-done((bf16[8,272,256]{2,1,0:T(8,128)(2,1)S(1)}, bf16[8,272,256]{2,1,0:T(8,128)(2,1)}, u32[]{:S(2)}) %copy-start.2) | copy-done | bytes 1114136
  29.8 0.0 copy-start.3
  29.8 1.2 %copy-done.3 = bf16[4,2,256,256]{3,2,1,0:T(8,128)(2,1)S(1)} copy-done((bf16[4,2,256,256]{3,2,1,0:T(8,128)(2,1)S(1)}, bf16[4,2,256,256]{3,2,1,0:T(8,128)(2,1)}, u32[]{:S(2)}) %copy-start.3) | copy-done | bytes 1048600
  31.0 0.0 copy-start.6
  31.0 0.7 %copy-done.6 = s32[2]{0:T(128)S(1)} copy-done((s32[2]{0:T(128)S(1)}, s32[2]{0:T(128)}, u32[]{:S(2)}) %copy-start.6) | copy-done | bytes 32
  31.7 8.9 %attend.1 = (bf16[2,1536,256]{2,1,0:T(8,128)(2,1)}, bf16[2,1536,256]{2,1,0:T(8,128)(2,1)}, bf16[4,2,256,256]{3,2,1,0:T(8,128)(2,1)S(1)}, f32[4,2,8,256]{3,2,1,0:T(8,128)S(1)}) custom-call(s32[8,2]{1,0:T(8,128)S(1)} %bitcast.2, s32[2]{0:T(128)S(1)} %copy-done.6, bf16[8,272,256]{2,1,0:T(8,128)(2,1)S(1)} %copy-done.2, ...), custom_call_target="tpu_custom_call" | custom-call | tf_op jit(solution)/shard_map/attend/pallas_call | solution.py:378
  40.6 0.0 copy-start.4
  40.6 1.0 %copy-done.4 = bf16[4,2,256,256]{3,2,1,0:T(8,128)(2,1)} copy-done((bf16[4,2,256,256]{3,2,1,0:T(8,128)(2,1)}, bf16[4,2,256,256]{3,2,1,0:T(8,128)(2,1)S(1)}, u32[]{:S(2)}) %copy-start.4) | copy-done | bytes 1048600
  41.6 0.0 copy-start.5
  41.6 0.6 %copy-done.5 = f32[4,2,8,256]{3,2,1,0:T(8,128)} copy-done((f32[4,2,8,256]{3,2,1,0:T(8,128)}, f32[4,2,8,256]{3,2,1,0:T(8,128)S(1)}, u32[]{:S(2)}) %copy-start.5) | copy-done | bytes 65560
  42.2 18.0 %combine.1 = bf16[2,256,256]{2,1,0:T(8,128)(2,1)} custom-call(bf16[4,2,256,256]{3,2,1,0:T(8,128)(2,1)} %copy-done.4, f32[4,2,8,256]{3,2,1,0:T(8,128)} %copy-done.5, s32[2]{0:T(128)} %active_ref.1), custom_call_target="tpu_custom_call" | custom-call | tf_op jit(solution)/shard_map/combine/pallas_call | solution.py:410
  60.2 1.7 %copy.18 = bf16[2,256,256]{2,1,0:T(8,128)(2,1)} copy(bf16[2,256,256]{2,1,0:T(8,128)(2,1)} %combine.1) | data formatting | bytes 524288
Async XLA Ops:
  25.7 1.4 %copy-start = (bf16[2,1536,256]{2,1,0:T(8,128)(2,1)S(1)}, bf16[2,1536,256]{2,1,0:T(8,128)(2,1)}, u32[]{:S(2)}) copy-start(bf16[2,1536,256]{2,1,0:T(8,128)(2,1)} %keys_ref.1) | copy-start | bytes 4718596
  27.1 1.4 %copy-start.1 = (bf16[2,1536,256]{2,1,0:T(8,128)(2,1)S(1)}, bf16[2,1536,256]{2,1,0:T(8,128)(2,1)}, u32[]{:S(2)}) copy-start(bf16[2,1536,256]{2,1,0:T(8,128)(2,1)} %values_ref.1) | copy-start | bytes 4718596
  28.5 1.2 %copy-start.2 = (bf16[8,272,256]{2,1,0:T(8,128)(2,1)S(1)}, bf16[8,272,256]{2,1,0:T(8,128)(2,1)}, u32[]{:S(2)}) copy-start(bf16[8,272,256]{2,1,0:T(8,128)(2,1)} %get-tuple-element.9.rows_ref) | copy-start | bytes 3342340
  29.8 1.2 %copy-start.3 = (bf16[4,2,256,256]{3,2,1,0:T(8,128)(2,1)S(1)}, bf16[4,2,256,256]{3,2,1,0:T(8,128)(2,1)}, u32[]{:S(2)}) copy-start(bf16[4,2,256,256]{3,2,1,0:T(8,128)(2,1)} %get-tuple-element.10.queries_ref) | copy-start | bytes 3145732
  31.0 0.7 %copy-start.6 = (s32[2]{0:T(128)S(1)}, s32[2]{0:T(128)}, u32[]{:S(2)}) copy-start(s32[2]{0:T(128)} %hist_ref.1) | copy-start | bytes 28
  40.6 1.0 %copy-start.4 = (bf16[4,2,256,256]{3,2,1,0:T(8,128)(2,1)}, bf16[4,2,256,256]{3,2,1,0:T(8,128)(2,1)S(1)}, u32[]{:S(2)}) copy-start(bf16[4,2,256,256]{3,2,1,0:T(8,128)(2,1)S(1)} %get-tuple-element.13.part_ref) | copy-start | bytes 3145732
  41.6 0.6 %copy-start.5 = (f32[4,2,8,256]{3,2,1,0:T(8,128)}, f32[4,2,8,256]{3,2,1,0:T(8,128)S(1)}, u32[]{:S(2)}) copy-start(f32[4,2,8,256]{3,2,1,0:T(8,128)S(1)} %get-tuple-element.14.stat_ref) | copy-start | bytes 196612

commit v2 on v1

v2 whole, which is shorter than its diff:
```python
import functools
import math

import jax
import jax.numpy as jnp
from jax import lax
from jax.experimental import pallas as pl
from jax.experimental.pallas import tpu as pltpu
from jax.sharding import PartitionSpec as P

MESH = pl.DeviceIdType.MESH
NT = (((1,), (1,)), ((), ()))
TAIL = 16


def pos_peers():
    p = lax.axis_index("pos")
    near = p + 1 - 2 * lax.rem(p, 2)
    far = lax.rem(p + 2, 4)
    return p, near, far


def merged_kernel(
    groups, blocks, users_here, cap, scale,
    owners_ref, hist_ref, active_ref, events_hbm, cand_hbm, keys_hbm, values_hbm,
    w_key_hbm, w_value_hbm,
    rows_hbm, counts_ref, out_ref,
    events_ref, queries, keys_ref, values_ref, weight_ref, rows_ref, packed, flipped, eye,
    acc, stat, near_out, near_part, near_stat, far_out, far_stat_out, far_part, far_stat,
    load_sem, rows_sem, a2a_send, a2a_recv, hop_send, hop_recv, q_send, q_recv,
    near_send, near_recv, far_send, far_recv,
):
    me = lax.axis_index("user")
    p, near, far = pos_peers()
    low, high = lax.rem(p, 2), p // 2
    cross = 2 * (1 - high) + 1 - low
    count = groups // blocks
    first = lax.rem(p - me + blocks * groups, blocks)
    far_first = lax.rem(far - me + blocks * groups, blocks)
    peers = [first + blocks * k for k in range(count)]
    block_rows, width = keys_ref.shape[1:]
    quarter = queries.shape[2]

    def load(src, dst, n):
        copy = pltpu.make_async_copy(src, dst, load_sem.at[n])
        copy.start()
        return copy

    own_q = load(cand_hbm, queries.at[p], 0)
    events_in = load(events_hbm, events_ref, 1)
    keys_in = load(keys_hbm, keys_ref, 2)
    values_in = load(values_hbm, values_ref, 3)
    weights_in = [load(w_key_hbm, weight_ref.at[0], 4), load(w_value_hbm, weight_ref.at[1], 5)]

    barrier = pltpu.get_barrier_semaphore()
    for peer in (near, far):
        pl.semaphore_signal(barrier, inc=1, device_id={"pos": peer}, device_id_type=MESH)
    for peer in peers:
        @pl.when(peer != me)
        def _():
            pl.semaphore_signal(barrier, inc=1, device_id={"user": peer}, device_id_type=MESH)

    per_event = events_ref.shape[0]
    features = events_ref.shape[1]
    users = groups * users_here
    owner = owners_ref[...]
    user_id = lax.broadcasted_iota(jnp.int32, (users, per_event), 0)
    same = (user_id == owner).astype(jnp.float32)
    before = (
        lax.broadcasted_iota(jnp.int32, (per_event, per_event), 0)
        <= lax.broadcasted_iota(jnp.int32, (per_event, per_event), 1)
    ).astype(jnp.float32).astype(jnp.bfloat16)
    ranks = jnp.dot(same.astype(jnp.bfloat16), before, preferred_element_type=jnp.float32)
    counts = jnp.sum(same, axis=1, keepdims=True)
    dest = owner // users_here
    earlier = (user_id >= dest * users_here) & (user_id < owner)
    slot = jnp.sum(jnp.where(earlier, counts, 0.0) + same * ranks, axis=0, keepdims=True) - 1.0
    slot = slot.astype(jnp.int32)
    slot_id = lax.broadcasted_iota(jnp.int32, (cap, per_event), 0)
    lane = lax.broadcasted_iota(jnp.int32, (users, features), 1)
    lane_user = lax.broadcasted_iota(jnp.int32, (users, features), 0)

    itself = (lax.rem(me, blocks) == first).astype(jnp.int32)
    pl.semaphore_wait(barrier, 2 + count - itself)

    def hop(ref_src, ref_dst, send, recv, peer):
        return pltpu.make_async_remote_copy(
            src_ref=ref_src, dst_ref=ref_dst, send_sem=send, recv_sem=recv,
            device_id={"pos": peer}, device_id_type=MESH,
        )

    own_q.wait()
    q_far = hop(queries.at[p], queries.at[p], q_send.at[0], q_recv.at[0], far)
    q_far.start()
    q_near = hop(queries.at[p], queries.at[p], q_send.at[1], q_recv.at[1], near)
    q_near.start()
    q_across = hop(queries.at[far], queries.at[far], q_send.at[2], q_recv.at[2], near)

    def a2a(k, peer, at):
        return pltpu.make_async_remote_copy(
            src_ref=packed.at[k], dst_ref=rows_ref.at[me],
            send_sem=a2a_send.at[k], recv_sem=a2a_recv.at[at],
            device_id={"user": peer}, device_id_type=MESH,
        )

    def own(k):
        return pltpu.make_async_copy(packed.at[k], rows_ref.at[me], load_sem.at[6 + k])

    events_in.wait()
    for k, peer in enumerate(peers):
        wanted = jnp.where(dest == peer, slot, -1)
        pick = (wanted == slot_id).astype(jnp.float32).astype(jnp.bfloat16)
        packed[k, :cap, :] = jnp.dot(
            pick, events_ref[...], preferred_element_type=jnp.float32
        ).astype(jnp.bfloat16)
        row = jnp.sum(
            jnp.where(lane_user == lane + peer * users_here, counts, 0.0), axis=0, keepdims=True
        )
        packed[k, cap:, :] = jnp.broadcast_to(row, (TAIL, features)).astype(jnp.bfloat16)

        @pl.when(peer != me)
        def _():
            a2a(k, peer, me // blocks).start()

        @pl.when(peer == me)
        def _():
            own(k).start()

    eye[...] = (
        lax.broadcasted_iota(jnp.int32, (width, width), 0)
        == lax.broadcasted_iota(jnp.int32, (width, width), 1)
    ).astype(jnp.float32).astype(jnp.bfloat16)
    factor = scale * math.log2(math.e)
    position = lax.broadcasted_iota(jnp.int32, (block_rows, quarter), 0) + p * block_rows
    keys_in.wait()
    values_in.wait()

    def flip(rows):
        return lax.dot_general(
            eye[...], rows, NT, preferred_element_type=jnp.float32
        ).astype(jnp.bfloat16)

    for u in range(users_here):
        flipped[u] = flip(values_ref[u])

    def keep(c, u, top, total):
        stat[c, u] = jnp.concatenate(
            [jnp.broadcast_to(top, (4, quarter)), jnp.broadcast_to(total, (4, quarter))], axis=0
        )

    def old_part(c):
        def one(u, carry):
            scores = lax.dot_general(
                keys_ref[u], queries[c, u], NT, preferred_element_type=jnp.float32
            ) * factor
            scores = jnp.where(position < hist_ref[u], scores, -1e30)
            top = jnp.maximum(jnp.max(scores, axis=0, keepdims=True), -1e29)
            expo = jnp.exp2(scores - top)
            keep(c, u, top, jnp.sum(expo, axis=0, keepdims=True))
            acc[c, u] = jnp.dot(
                flipped[u], expo.astype(jnp.bfloat16), preferred_element_type=jnp.float32
            )
            return carry

        lax.fori_loop(0, users_here, one, 0)

    old_part(p)
    q_near.wait_recv()
    old_part(near)
    q_far.wait_recv()
    q_across.start()
    old_part(far)
    q_across.wait_recv()
    old_part(cross)

    def forward(stage, k, start, peer):
        block = rows_ref.at[start + blocks * k]
        return hop(block, block, hop_send.at[stage, k], hop_recv.at[stage, k], peer)

    for k, peer in enumerate(peers):
        @pl.when(peer != me)
        def _():
            a2a(k, peer, k).wait_recv()

        @pl.when(peer == me)
        def _():
            own(k).wait()

        forward(0, k, first, far).start()
        forward(1, k, first, near).start()
    for copy in weights_in:
        copy.wait()
    keys_new, flipped_new, masks = [], [], []
    slots = lax.broadcasted_iota(jnp.int32, (cap, quarter), 0).astype(jnp.float32)
    for k, peer in enumerate(peers):
        raw = rows_ref[peer, :cap, :]
        made = [
            jnp.dot(raw, weight_ref[i], preferred_element_type=jnp.float32).astype(jnp.bfloat16)
            for i in range(2)
        ]
        keys_new.append(made[0])
        flipped_new.append(flip(made[1]))
        tail = rows_ref[peer, cap:, :].astype(jnp.float32)
        begin = jnp.zeros((1, 1), jnp.float32)
        mask = []
        for u in range(users_here):
            end = begin + tail[0:1, u : u + 1]
            mask.append((slots >= begin) & (slots < end))
            begin = end
        masks.append(mask)
    keys_new = jnp.concatenate(keys_new, axis=0)
    flipped_new = jnp.concatenate(flipped_new, axis=1)
    masks = [jnp.concatenate([m[u] for m in masks], axis=0) for u in range(users_here)]

    def new_part(c, u):
        scores = lax.dot_general(
            keys_new, queries[c, u], NT, preferred_element_type=jnp.float32
        ) * factor
        scores = jnp.where(masks[u], scores, -1e30)
        old = stat[c, u]
        top = jnp.maximum(jnp.max(scores, axis=0, keepdims=True), old[0:1])
        expo = jnp.exp2(scores - top)
        shrink = jnp.exp2(old[0:1] - top)
        total = old[4:5] * shrink + jnp.sum(expo, axis=0, keepdims=True)
        part = acc[c, u] * shrink + jnp.dot(
            flipped_new, expo.astype(jnp.bfloat16), preferred_element_type=jnp.float32
        )
        return top, total, part

    def copies(pairs, send, recv, n, peer):
        return [
            hop(src, dst, send.at[i, n], recv.at[i, n], peer)
            for i, (src, dst) in enumerate(pairs)
        ]

    first_copies = {}
    for h, c in enumerate((cross, near)):
        for u in range(users_here):
            top, total, part = new_part(c, u)
            near_out[h, u] = part.astype(jnp.bfloat16)
            keep(c, u, top, total)
            first_copies[h, u] = copies(
                ((near_out.at[h, u], near_part.at[h, u]), (stat.at[c, u], near_stat.at[h, u])),
                near_send, near_recv, h * users_here + u, near,
            )
            for copy in first_copies[h, u]:
                copy.start()

    def merge(top, total, part, other, other_part):
        new_top = jnp.maximum(top, other[0:1])
        mine = jnp.exp2(top - new_top)
        theirs = jnp.exp2(other[0:1] - new_top)
        total = total * mine + other[4:5] * theirs
        return new_top, total, part * mine + other_part.astype(jnp.float32) * theirs

    def near_merged(h, c, u):
        top, total, part = new_part(c, u)
        for copy in first_copies[h, u]:
            copy.wait_recv()
        return merge(top, total, part, near_stat[h, u], near_part[h, u])

    second = []
    for u in range(users_here):
        top, total, part = near_merged(0, far, u)
        far_out[u] = part.astype(jnp.bfloat16)
        far_stat_out[u] = jnp.concatenate(
            [jnp.broadcast_to(top, (4, quarter)), jnp.broadcast_to(total, (4, quarter))], axis=0
        )
        second.append(
            copies(
                ((far_out.at[u], far_part.at[u]), (far_stat_out.at[u], far_stat.at[u])),
                far_send, far_recv, u, far,
            )
        )
        for copy in second[u]:
            copy.start()
    for u in range(users_here):
        top, total, part = near_merged(1, p, u)
        acc[p, u] = part
        keep(p, u, top, total)

    for k in range(count):
        forward(0, k, first, far).wait_recv()
        forward(2, k, far_first, near).start()
    for k in range(count):
        forward(1, k, first, near).wait_recv()
        forward(2, k, far_first, near).wait_recv()
    stored = pltpu.make_async_copy(rows_ref, rows_hbm, rows_sem)
    stored.start()
    for g in range(groups):
        counts_ref[g : g + 1, :] = rows_ref[g, cap : cap + TAIL, :128].astype(jnp.float32)[
            0:1
        ].astype(jnp.int32)

    for u in range(users_here):
        for copy in second[u]:
            copy.wait_recv()
        mine = stat[p, u]
        top, total, part = merge(mine[0:1], mine[4:5], acc[p, u], far_stat[u], far_part[u])
        flag = active_ref[u].astype(jnp.float32)
        out_ref[u] = (part * (flag / total)).T.astype(jnp.bfloat16)
    stored.wait()
    for copy in (q_far, q_near, q_across):
        copy.wait_send()
    for group in list(first_copies.values()) + second:
        for copy in group:
            copy.wait_send()
    for k, peer in enumerate(peers):
        @pl.when(peer != me)
        def _():
            a2a(k, peer, k).wait_send()

        forward(0, k, first, far).wait_send()
        forward(1, k, first, near).wait_send()
        forward(2, k, far_first, near).wait_send()


def place_kernel(
    groups, cap,
    count_ref, hist_ref, rows_ref, w_key_ref, w_value_ref, keys_ref, values_ref, attended_ref,
    new_keys_ref, new_values_ref, out_ref,
    made, fresh,
):
    user = pl.program_id(0)
    step = pl.program_id(1)
    steps = pl.num_programs(1)
    rows = keys_ref.shape[1]
    width = keys_ref.shape[2]

    @pl.when((user == 0) & (step == 0))
    def _():
        def project(g, carry):
            for i, weight in enumerate((w_key_ref, w_value_ref)):
                made[g, :, i * width : (i + 1) * width] = jnp.dot(
                    rows_ref[g, :cap, :], weight[...], preferred_element_type=jnp.float32
                ).astype(jnp.bfloat16)
            return carry

        lax.fori_loop(0, groups, project, 0)

    out_ref[...] = attended_ref[...]
    origin = (lax.axis_index("pos") * steps + step) * rows
    start = hist_ref[user] - origin
    limit = lax.fori_loop(0, groups, lambda g, n: n + count_ref[g, user], start)
    touched = (limit > 0) & (start < rows) & (limit > start)

    @pl.when(jnp.logical_not(touched))
    def _():
        new_keys_ref[...] = keys_ref[...]
        new_values_ref[...] = values_ref[...]

    @pl.when(touched)
    def _():
        fresh[...] = jnp.zeros_like(fresh)
        gap = lax.broadcasted_iota(jnp.int32, (rows, cap), 1) - lax.broadcasted_iota(
            jnp.int32, (rows, cap), 0
        )
        slot = lax.broadcasted_iota(jnp.int32, (rows, cap), 1)

        def place(g, at):
            size = count_ref[g, user]

            @pl.when((size > 0) & (at < rows) & (at + size > 0))
            def _():
                low = lax.fori_loop(0, user, lambda j, n: n + count_ref[g, j], 0)
                pick = (gap == low - at) & (slot >= low) & (slot < low + size)
                fresh[...] += jnp.dot(
                    pick.astype(jnp.float32).astype(jnp.bfloat16), made[g],
                    preferred_element_type=jnp.float32,
                )

            return at + size

        lax.fori_loop(0, groups, place, start)
        row = lax.broadcasted_iota(jnp.int32, (rows, width), 0)
        inside = (row >= start) & (row < limit)
        new_keys_ref[0] = jnp.where(
            inside, fresh[:, :width], keys_ref[0].astype(jnp.float32)
        ).astype(jnp.bfloat16)
        new_values_ref[0] = jnp.where(
            inside, fresh[:, width:], values_ref[0].astype(jnp.float32)
        ).astype(jnp.bfloat16)


def on_device(
    events, owners, offsets, w_key, w_value, cache_keys, cache_values, hist_len, active, candidates
):
    groups = lax.axis_size("user")
    blocks = lax.axis_size("pos")
    users_here, block_rows, width = cache_keys.shape
    per_event, features = events.shape
    cap = 2 * per_event // groups
    quarter = candidates.shape[1]
    count = groups // blocks
    vmem = pl.BlockSpec(memory_space=pltpu.VMEM)
    smem = pl.BlockSpec(memory_space=pltpu.SMEM)
    hbm = pl.BlockSpec(memory_space=pl.ANY)
    dma = pltpu.SemaphoreType.DMA
    bf16, f32 = jnp.bfloat16, jnp.float32

    rows, counts, attended = pl.pallas_call(
        functools.partial(merged_kernel, groups, blocks, users_here, cap, width ** -0.5),
        out_shape=(
            jax.ShapeDtypeStruct((groups, cap + TAIL, features), bf16),
            jax.ShapeDtypeStruct((groups, 128), jnp.int32),
            jax.ShapeDtypeStruct(candidates.shape, bf16),
        ),
        in_specs=[vmem, smem, smem] + [hbm] * 6,
        out_specs=(hbm, vmem, vmem),
        scratch_shapes=[
            pltpu.VMEM(events.shape, bf16),
            pltpu.VMEM((blocks,) + candidates.shape, bf16),
            pltpu.VMEM(cache_keys.shape, bf16),
            pltpu.VMEM(cache_values.shape, bf16),
            pltpu.VMEM((2, features, width), bf16),
            pltpu.VMEM((groups, cap + TAIL, features), bf16),
            pltpu.VMEM((count, cap + TAIL, features), bf16),
            pltpu.VMEM((users_here, width, block_rows), bf16),
            pltpu.VMEM((width, width), bf16),
            pltpu.VMEM((blocks, users_here, width, quarter), f32),
            pltpu.VMEM((blocks, users_here, 8, quarter), f32),
            pltpu.VMEM((2, users_here, width, quarter), bf16),
            pltpu.VMEM((2, users_here, width, quarter), bf16),
            pltpu.VMEM((2, users_here, 8, quarter), f32),
            pltpu.VMEM((users_here, width, quarter), bf16),
            pltpu.VMEM((users_here, 8, quarter), f32),
            pltpu.VMEM((users_here, width, quarter), bf16),
            pltpu.VMEM((users_here, 8, quarter), f32),
            dma((6 + count,)), dma, dma((count,)), dma((count,)),
            dma((3, count)), dma((3, count)), dma((3,)), dma((3,)),
            dma((2, 2 * users_here)), dma((2, 2 * users_here)),
            dma((2, users_here)), dma((2, users_here)),
        ],
        compiler_params=pltpu.CompilerParams(
            collective_id=0, has_side_effects=True, vmem_limit_bytes=60 * 2**20
        ),
        name="merged",
    )(
        owners.reshape(1, per_event), hist_len, active, events, candidates,
        cache_keys, cache_values, w_key, w_value,
    )

    step_rows = block_rows // 3
    cache_spec = pl.BlockSpec((1, step_rows, width), lambda u, b: (u, b, 0))
    read_spec = pl.BlockSpec((1, quarter, width), lambda u, b: (u, 0, 0))
    return pl.pallas_call(
        functools.partial(place_kernel, groups, cap),
        grid=(users_here, block_rows // step_rows),
        out_shape=(
            jax.ShapeDtypeStruct(cache_keys.shape, bf16),
            jax.ShapeDtypeStruct(cache_values.shape, bf16),
            jax.ShapeDtypeStruct(candidates.shape, bf16),
        ),
        in_specs=[smem, smem, vmem, vmem, vmem, cache_spec, cache_spec, read_spec],
        out_specs=(cache_spec, cache_spec, read_spec),
        scratch_shapes=[
            pltpu.VMEM((groups, cap, 2 * width), bf16),
            pltpu.VMEM((step_rows, 2 * width), f32),
        ],
        compiler_params=pltpu.CompilerParams(
            dimension_semantics=("arbitrary", "arbitrary"), vmem_limit_bytes=60 * 2**20
        ),
        name="place",
    )(counts, hist_len, rows, w_key, w_value, cache_keys, cache_values, attended)


def solution(mesh):
    placed = (
        P("user", None),
        P("user"),
        P("user"),
        P(),
        P(),
        P("user", "pos", None),
        P("user", "pos", None),
        P("user"),
        P("user"),
        P("user", "pos", None),
    )
    return jax.shard_map(
        on_device,
        mesh=mesh,
        in_specs=placed,
        out_specs=(P("user", "pos", None), P("user", "pos", None), P("user", "pos", None)),
        check_vma=False,
    )
```

time: 62.5 us -> 47.8 us (0.76); the launches traced: 61.9 us -> 48.2 us
  local copies, waits for them, and re-layouts: 9.2 us -> 0 us
  Pallas kernels: 50.3 us -> 47.6 us
  other arithmetic: 1.71 us -> 0 us
    unnamed x15 -> x0, local copies, waits for them, and re-layouts: 9.2 us -> none
    pallas_call x3 -> x2, Pallas kernels: 50.3 us -> 47.6 us  [the longest x1 33.9 us: on_device(): pl.pallas_call(functools.partial(merged_kernel, groups, blocks, users_her...]
    concatenate x1 -> x0, other arithmetic: 0.99 us -> none  [on_device(): weights = jnp.concatenate([w_key, w_value], axis=1)]
    convert_element_type x1 -> x0, other arithmetic: 0.72 us -> none  [on_device(): counts = rows[:, cap, :users_here].astype(jnp.int32)]
where the time goes in v2:
time: 47.8 us; the launch traced here: 48.2 us
  Pallas kernels  47.6 us (100%)
  between operations  0.64 us (1%)
    pallas_call x1, Pallas kernels, on_device(): pl.pallas_call(functools.partial(merged_kernel, groups, blocks, users_her...  33.9 us
    pallas_call x1, Pallas kernels, on_device(): pl.pallas_call(functools.partial(place_kernel, groups, cap), grid=(users_...  13.7 us

profile of v2, /device:TPU:1, one launch (start us, length us, event | category | flops | bytes accessed | tf_op | source)
XLA Modules:
  0.0 48.2 jit_solution(11325959638285960223)
XLA Ops:
  0.6 33.9 %merged.1 = (bf16[8,272,256]{2,1,0:T(8,128)(2,1)}, s32[8,128]{1,0:T(8,128)}, bf16[2,256,256]{2,1,0:T(8,128)(2,1)}) custom-call(s32[1,1024]{1,0:T(1,128)} %bitcast.1, s32[2]{0:T(128)} %hist_ref.3, s32[2]{0:T(128)} %active_ref.1, bf16[1024,256]{1,0:T(8,128)(2,1)} %events_hbm.1, bf16[2,256,256]{2,1,0:T(8,128)(2,1)} %cand_hbm.1, bf16[2,1536,256]{2,1,0:T(8,128)(2,1)} %keys_ref.1, ...), custom_call_target="tpu_custom_call" | custom-call | tf_op jit(solution)/shard_map/merged/pallas_call | solution.py:401
  34.5 13.7 %place.1 = (bf16[2,1536,256]{2,1,0:T(8,128)(2,1)}, bf16[2,1536,256]{2,1,0:T(8,128)(2,1)}, bf16[2,256,256]{2,1,0:T(8,128)(2,1)}) custom-call(s32[8,128]{1,0:T(8,128)} %get-tuple-element.6.count_ref, s32[2]{0:T(128)} %hist_ref.3, bf16[8,272,256]{2,1,0:T(8,128)(2,1)} %get-tuple-element.7.rows_ref, bf16[256,256]{1,0:T(8,128)(2,1)} %w_key_ref.1, ...), custom_call_target="tpu_custom_call" | custom-call | tf_op jit(solution)/shard_map/place/pallas_call | solution.py:446
